TPU v7x, 512 devices: a whole 4x8x8 slice. The times are simulated.
512 devices in a mesh: pop: 32 (over y_lo, x, core), tp: 16 (over z, y_hi).
Axes of the slice: x: 4, y: 8 (y_hi: 2, y_lo: 4; y = y_hi * 4 + y_lo), z: 8, core: 2. Of those that a mesh axis runs over, the one named last changes fastest.
Arguments:
- tokens: bfloat16 [16384, 8192], P('pop', 'tp'), may hold values from -6 to 6
- weight: bfloat16 [8192, 8192], P('pop', 'tp'), may hold values from -0.0625 to 0.0625
- left: bfloat16 [512, 8192], P('pop', 'tp'), may hold values from -0.0625 to 0.0625
- right: bfloat16 [512, 8192], P('pop', 'tp'), may hold values from -6 to 6
- target: bfloat16 [16384, 8192], P('pop', 'tp'), may hold values from -6 to 6
Outputs:
- hidden: bfloat16 [16384, 8192], P('pop', 'tp')
- update: float32 [8192, 8192], P('pop', 'tp')
All inputs are finite; a program needn't handle non-finite values.
Results may differ from a plain program's by a relative error of at most 0.001.
Values may be sent and summed in bfloat16 or wider, within the bound.
A program may use at most 128 MiB of HBM per device.

v0:
```python
import jax
import jax.numpy as jnp
from jax import lax
from jax.sharding import PartitionSpec as P

D = 8192


sigma_scale = 0.5
epsilon = 1e-06


def side_by_side(arrays, axis, dim, along):
    both = jnp.concatenate(arrays, axis=along)
    filled, at, finished = (lax.all_gather(both, axis, axis=dim, tiled=True), 0, [])
    for a in arrays:
        finished.append(lax.slice_in_dim(filled, at, at + a.shape[along], axis=along))
        at += a.shape[along]
    return tuple(finished)


def copy_for_each(x, axis):
    length = lax.axis_size(axis)
    return lax.all_to_all(jnp.broadcast_to(x[None], (length, *x.shape)), axis, 0, 0, tiled=True)


def over_copies(x, axis):
    everything = copy_for_each(x, axis)
    return jnp.sum(everything, axis=0)


def laid_out(tiles, dim):
    dims = list(tiles.shape[1:])
    dims[dim] *= tiles.shape[0]
    return jnp.moveaxis(tiles, 0, dim).reshape(dims)


def gathered_copies(x, axis, dim):
    return laid_out(copy_for_each(x, axis), dim)


def per_device(tokens, weight, left, right, target):
    members = left.shape[0]
    length = tokens.shape[0] // members
    columns = tokens.shape[1]
    whole_tok, whole_left = side_by_side((tokens, left), "tp", 1, 0)
    full_weight = lax.all_gather(weight, "pop", axis=0, tiled=True)
    base = jnp.dot(whole_tok, full_weight, preferred_element_type=jnp.float32)
    grouped = whole_tok.reshape(members, length, whole_tok.shape[1])
    scores = jnp.einsum("mld,md->ml", grouped, whole_left, preferred_element_type=jnp.float32)
    own_tok = tokens.astype(jnp.float32).reshape(members, length, columns)
    full = (
        base.reshape(members, length, columns)
        + sigma_scale * scores[:, :, None] * right.astype(jnp.float32)[:, None, :]
        + own_tok
    )
    hidden = full.astype(jnp.bfloat16).reshape(members * length, columns)
    differ = full - target.astype(jnp.float32).reshape(members, length, columns)
    partial_loss = jnp.sum(differ * differ, axis=(1, 2))
    own_loss = over_copies(partial_loss, "tp")
    losses = gathered_copies(own_loss, "pop", 0) / (length * D)
    mean = jnp.mean(losses)
    spread = jnp.mean(losses * losses) - mean * mean
    fitness = -(losses - mean) / jnp.sqrt(spread + epsilon)
    owned_left = lax.all_to_all(whole_left, "pop", split_axis=1, concat_axis=0, tiled=True)
    owned_right = gathered_copies(right, "pop", 0)
    weighted = fitness[:, None] * owned_left.astype(jnp.float32)
    update = jnp.dot(weighted.T, owned_right.astype(jnp.float32), precision=lax.Precision.HIGHEST)
    update = update / (losses.shape[0] * sigma_scale)
    return (hidden, update)


def solution(mesh):
    return jax.shard_map(
        per_device,
        mesh=mesh,
        in_specs=(P("pop", "tp"), P("pop", "tp"), P("pop", "tp"), P("pop", "tp"), P("pop", "tp")),
        out_specs=(P("pop", "tp"), P("pop", "tp")),
        check_vma=False,
    )
```

profile of v0, /device:TPU:1, one launch (start us, length us, event | category | flops | bytes accessed | tf_op | source)
XLA Modules:
  0.0 386.1 jit_solution(550260012578329019)
XLA Ops:
  7.2 0.0 all-gather.3.cloned.1.call-start
  7.2 1.9 pad_maximum_fusion
  9.1 0.0 all-gather.3.cloned.1.call-update
  9.1 0.0 all-gather.5.cloned.1.call-start
  9.2 0.7 all-gather.5.cloned.1.call-update
  9.9 1.3 copy.32
  11.2 0.8 mul.53
  12.0 0.3 copy.31
  12.3 1.3 copy.33
  13.6 210.5 %all-gather.3.cloned.1.call-done = bf16[528,8192]{1,0:T(8,128)(2,1)} async-done(((bf16[528,512]{1,0:T(8,128)(2,1)}), bf16[528,8192]{1,0:T(8,128)(2,1)}) %all-gather.3.cloned.1.call-update) | async-done | bytes 8650768 | tf_op jit(solution)/shard_map/all_gather | solution.py:15
  224.1 7.6 %slice.8 = bf16[512,8192]{1,0:T(8,128)(2,1)} slice(bf16[528,8192]{1,0:T(8,128)(2,1)} %all-gather.3.cloned.1.call-done), slice={[0:512], [0:8192]} | slice | bytes 16777216 | tf_op jit(solution)/shard_map/slice | solution.py:17
  231.7 1.0 fusion.8
  232.7 5.6 %fusion.2 = f32[16,1,32]{2,1,0:T(1,128)S(1)} fusion(bf16[16,32,8192]{2,1,0:T(8,128)(2,1)} %bitcast.22, bf16[16,8192,1]{1,0,2:T(8,128)(2,1)S(1)} %get-tuple-element.17), kind=kOutput, calls=%fused_computation.7 | convolution fusion | flops 8388608 | bytes 8652800 | tf_op jit(solution)/shard_map/mld,md->ml/dot_general | solution.py:50
  238.3 0.1 mul.51
  238.4 0.0 copy-start
  238.4 55.8 %all-gather.5.cloned.1.call-done = bf16[8192,512]{1,0:T(8,128)(2,1)} async-done(((bf16[256,512]{1,0:T(8,128)(2,1)}), bf16[8192,512]{1,0:T(8,128)(2,1)}) %all-gather.5.cloned.1.call-update) | async-done | bytes 8388624 | tf_op jit(solution)/shard_map/all_gather | solution.py:47
  294.2 10.5 %multiply_reduce_fusion = (f32[512]{0:T(512)S(1)}, bf16[512,512]{0,1:T(8,128)(2,1)S(1)}) fusion(bf16[512,512]{0,1:T(8,128)(2,1)S(1)} %copy.33, bf16[512,512]{0,1:T(8,128)(2,1)S(1)} %copy.32, f32[512,512]{0,1:T(8,128)S(1)} %copy.31, f32[512]{0:T(512)S(1)} %mul.51, bf16[8192,512]{1,0:T(8,128)(2,1)} %all-gather.5.cloned.1.call-done, ...), kind=kOutput, calls=%fused_computation.4 | convolution fusion | flops 4297326080 | bytes 19402752 | tf_op jit(solution)/shard_map/dot_general | solution.py:48
  304.6 0.1 reduce_sum.44
  304.7 0.1 reduce_sum.45
  304.9 22.0 %all_to_all.30 = f32[16,1,16]{2,1,0:T(1,128)S(1)} all-to-all(f32[16,1,16]{2,1,0:T(1,128)S(1)} %broadcast_in_dim.6), channel_id=1, replica_groups=mesh['pop'=32,'tp'=16] {'tp'}, dimensions={0} | all-to-all | bytes 2048 | tf_op jit(solution)/shard_map/all_to_all | solution.py:24
  326.8 0.0 copy-done
  326.8 0.9 broadcast_in_dim.8
  327.7 6.3 %all-to-all-start.3 = ((bf16[32,16,512]{2,1,0:T(8,128)(2,1)}), bf16[32,16,512]{2,1,0:T(8,128)(2,1)S(1)}, u32[]{:S(2)}, u32[]{:S(2)}) async-start(bf16[32,16,512]{2,1,0:T(8,128)(2,1)} %broadcast_in_dim.8), calls=%async_computation.3 | async-start | bytes 1048576 | tf_op jit(solution)/shard_map/all_to_all | solution.py:24
  334.0 16.4 %all-to-all-done.3 = bf16[32,16,512]{2,1,0:T(8,128)(2,1)S(1)} async-done(((bf16[32,16,512]{2,1,0:T(8,128)(2,1)}), bf16[32,16,512]{2,1,0:T(8,128)(2,1)S(1)}, u32[]{:S(2)}, u32[]{:S(2)}) %all-to-all-start.3) | async-done | bytes 524320 | tf_op jit(solution)/shard_map/all_to_all | solution.py:24
  350.4 0.6 broadcast_in_dim.7
  351.1 4.1 %all-to-all-start.1 = ((f32[32,1,16]{2,1,0:T(1,128)}), f32[32,1,16]{2,1,0:T(1,128)S(1)}, u32[]{:S(2)}, u32[]{:S(2)}) async-start(f32[32,1,16]{2,1,0:T(1,128)} %broadcast_in_dim.7), calls=%async_computation.1 | async-start | bytes 32768 | tf_op jit(solution)/shard_map/all_to_all | solution.py:24
  355.2 0.7 copy.43
  355.9 6.5 %all-to-all-done.1 = f32[32,1,16]{2,1,0:T(1,128)S(1)} async-done(((f32[32,1,16]{2,1,0:T(1,128)}), f32[32,1,16]{2,1,0:T(1,128)S(1)}, u32[]{:S(2)}, u32[]{:S(2)}) %all-to-all-start.1) | async-done | bytes 2080 | tf_op jit(solution)/shard_map/all_to_all | solution.py:24
  362.4 4.2 %all-to-all-start.2 = ((bf16[16,32,256]{2,0,1:T(8,128)(2,1)}), bf16[16,32,256]{2,0,1:T(8,128)(2,1)S(1)}, u32[]{:S(2)}, u32[]{:S(2)}) async-start(bf16[16,32,256]{2,0,1:T(8,128)(2,1)} %bitcast.21), calls=%async_computation.2 | async-start | bytes 524288 | tf_op jit(solution)/shard_map/all_to_all | solution.py:65
  366.6 1.0 copy.36
  367.6 0.7 fusion.6
  370.9 6.9 %all-to-all-done.2 = bf16[16,32,256]{2,0,1:T(8,128)(2,1)S(1)} async-done(((bf16[16,32,256]{2,0,1:T(8,128)(2,1)}), bf16[16,32,256]{2,0,1:T(8,128)(2,1)S(1)}, u32[]{:S(2)}, u32[]{:S(2)}) %all-to-all-start.2) | async-done | bytes 262176 | tf_op jit(solution)/shard_map/all_to_all | solution.py:65
  377.8 1.5 fusion.1
  (4 shorter events, 0.1 us)
Async XLA Ops:
  7.2 216.9 %all-gather.3.cloned.1.call-start = ((), (), s32[]{:S(2)}) async-start(), calls=%async_computation.4 | async-start | bytes 9191424 | tf_op jit(solution)/shard_map/all_gather | solution.py:15
  9.1 285.0 %all-gather.5.cloned.1.call-start = ((), (), s32[]{:S(2)}) async-start(), calls=%async_computation.5 | async-start | bytes 8650752 | tf_op jit(solution)/shard_map/all_gather | solution.py:47
  238.4 88.5 %copy-start = (bf16[16,512]{1,0:T(8,128)(2,1)S(1)}, bf16[16,512]{1,0:T(8,128)(2,1)}, u32[]{:S(2)}) copy-start(bf16[16,512]{1,0:T(8,128)(2,1)} %param.8) | copy-start | bytes 49156
  327.7 22.7 %all-to-all-start.3 = ((bf16[32,16,512]{2,1,0:T(8,128)(2,1)}), bf16[32,16,512]{2,1,0:T(8,128)(2,1)S(1)}, u32[]{:S(2)}, u32[]{:S(2)}) async-start(bf16[32,16,512]{2,1,0:T(8,128)(2,1)} %broadcast_in_dim.8), calls=%async_computation.3 | async-start | bytes 1048576 | tf_op jit(solution)/shard_map/all_to_all | solution.py:24
  351.1 11.4 %all-to-all-start.1 = ((f32[32,1,16]{2,1,0:T(1,128)}), f32[32,1,16]{2,1,0:T(1,128)S(1)}, u32[]{:S(2)}, u32[]{:S(2)}) async-start(f32[32,1,16]{2,1,0:T(1,128)} %broadcast_in_dim.7), calls=%async_computation.1 | async-start | bytes 32768 | tf_op jit(solution)/shard_map/all_to_all | solution.py:24
  362.4 15.4 %all-to-all-start.2 = ((bf16[16,32,256]{2,0,1:T(8,128)(2,1)}), bf16[16,32,256]{2,0,1:T(8,128)(2,1)S(1)}, u32[]{:S(2)}, u32[]{:S(2)}) async-start(bf16[16,32,256]{2,0,1:T(8,128)(2,1)} %bitcast.21), calls=%async_computation.2 | async-start | bytes 524288 | tf_op jit(solution)/shard_map/all_to_all | solution.py:65
Sparse Core Ops, SparseCore 0:
  11.0 212.9 all-gather.2
  226.2 67.9 all-gather.4
where the time goes:
time: 387 us; the launch traced here: 386 us
  waiting for transfers between devices  297 us (77%)
  blocking collectives  22 us (6%)
  matrix products  17.6 us (5%)
  between operations  16.7 us (4%)
  local copies, waits for them, and re-layouts  15.6 us (4%)
  starting transfers between devices  14.6 us (4%)
    all_gather x1, waiting for transfers between devices, side_by_side(): lax.all_gather(both, axis, axis=dim, tiled=True)  210 us
    all_gather x1, waiting for transfers between devices, per_device(): full_weight = lax.all_gather(weight, 'pop', axis=0, tiled=True)  55.8 us
    all_to_all x2, waiting for transfers between devices, copy_for_each(): lax.all_to_all(jnp.broadcast_to(x[None], (length, *x.shape)), axis, 0, 0,...  23 us
    all_to_all x1, blocking collectives, copy_for_each(): lax.all_to_all(jnp.broadcast_to(x[None], (length, *x.shape)), axis, 0, 0,...  22 us
    dot_general x1, matrix products, per_device(): base = jnp.dot(whole_tok, full_weight, preferred_element_type=jnp.float32)  10.5 us
    all_to_all x2, starting transfers between devices, copy_for_each(): lax.all_to_all(jnp.broadcast_to(x[None], (length, *x.shape)), axis, 0, 0,...  10.4 us
    slice x2, local copies, waits for them, and re-layouts, side_by_side(): lax.slice_in_dim(filled, at, at + a.shape[along], axis=along)  8.59 us
  transfers between devices with their start and end apart: 5, of which 5 were waited for; matrix products, arithmetic and copies ran while one was open for 5% of the time, Pallas kernels for 0%

commit v1 on v0

v1 whole, which is shorter than its diff:
```python
import functools

import jax
import jax.numpy as jnp
from jax import lax
from jax.experimental import pallas as pl
from jax.experimental.pallas import tpu as pltpu
from jax.sharding import PartitionSpec as P

D = 8192
LEN = 32
MEMBERS = 512

sigma_scale = 0.5
epsilon = 1e-06

MESH = pl.DeviceIdType.MESH
NX, NY, NYL, NZ = 4, 8, 4, 8
NPOP, NTP = 32, 16
ROWS = 512
COLS = 512
KB = 256
MEM = 16
TB = ROWS + MEM
WB = KB + MEM
HALF = 256
WHALF = 128


def kernel(
    tok_hbm, w_hbm, left_hbm, right_hbm, tgt_hbm, hid_hbm, upd_hbm,
    tokbuf, wbuf, relay_a, relay_b, acc, sc, tgt, hid, leftbuf, left_t, upd, loss1, loss2,
    loc, zs, zr, ys, yr, xs, xr, fs, fr, cs, cr, rs, rr, qs, qr, las, lar, t1s, t1r, t2s, t2r,
):
    p = lax.axis_index("pop")
    t = lax.axis_index("tp")
    core = p % 2
    x = (p // 2) % NX
    yl = p // (2 * NX)
    z = t // 2
    yh = t % 2
    y = yh * NYL + yl

    def pop_of(yl_, x_, c_):
        return (yl_ * NX + x_) * 2 + c_

    def at_y(y_):
        y_ = y_ % NY
        return (pop_of(y_ % NYL, x, core), z * 2 + y_ // NYL)

    def at_x(x_):
        return (pop_of(yl, x_ % NX, core), t)

    def at_z(z_):
        return (p, (z_ % NZ) * 2 + yh)

    other_core = (pop_of(yl, x, 1 - core), t)
    t_mate = z * 2 + (1 - yh)

    loads = [
        pltpu.make_async_copy(tok_hbm, tokbuf.at[t, pl.ds(0, ROWS)], loc.at[0]),
        pltpu.make_async_copy(left_hbm, tokbuf.at[t, pl.ds(ROWS, MEM)], loc.at[1]),
        pltpu.make_async_copy(w_hbm, wbuf.at[p, pl.ds(0, KB)], loc.at[2]),
        pltpu.make_async_copy(right_hbm, wbuf.at[p, pl.ds(KB, MEM)], loc.at[3]),
        pltpu.make_async_copy(tgt_hbm, tgt, loc.at[4]),
    ]
    for c in loads:
        c.start()

    barrier = pltpu.get_barrier_semaphore()
    near = [at_y(y + k + NY) for k in (1, -1, 2, -2, 3, -3)]
    near += [at_x(x + 1), at_x(x + NX - 1), at_z(z + 1), at_z(z + NZ - 1), other_core]
    for d in near:
        pl.semaphore_signal(barrier, inc=1, device_id=d, device_id_type=MESH)
    acc[...] = jnp.zeros_like(acc)
    sc[...] = jnp.zeros_like(sc)
    pl.semaphore_wait(barrier, len(near))

    def remote(src, dst, s, r, dev):
        return pltpu.make_async_remote_copy(
            src_ref=src, dst_ref=dst, send_sem=s, recv_sem=r, device_id=dev, device_id_type=MESH
        )

    sent = []

    def go(c):
        c.start()
        sent.append(c)

    def chunk(block, c):
        return tokbuf.at[block, pl.ds(0, HALF)] if c == 0 else tokbuf.at[block, pl.ds(HALF, TB - HALF)]

    def zcopy(ring, way, j):
        c = j % 2 if way == 0 else 1 - j % 2
        dist = j // 2
        src_z = z + NZ - dist if way == 0 else z + dist
        block = (src_z % NZ) * 2 + (yh if ring == 0 else 1 - yh)
        ref = chunk(block, c)
        dev = at_z(z + 1) if way == 0 else at_z(z + NZ - 1)
        return remote(ref, ref, zs.at[way, ring, j], zr.at[way, ring, j], dev)

    def zwait(ring, way, j):
        c = j % 2 if way == 0 else 1 - j % 2
        dist = j // 2 + 1
        src_z = z + NZ - dist if way == 0 else z + dist
        block = (src_z % NZ) * 2 + (yh if ring == 0 else 1 - yh)
        ref = chunk(block, c)
        dev = at_z(z + NZ - 1) if way == 0 else at_z(z + 1)
        remote(ref, ref, zs.at[way, ring, j], zr.at[way, ring, j], dev).wait_recv()

    def zevent(ring, j):
        for way in (0, 1):
            zwait(ring, way, j)
            if j + 2 < 7:
                go(zcopy(ring, way, j + 2))

    def wblock(k, dx):
        return pop_of((yl + NYL - k) % NYL, (x + dx + NX) % NX, core)

    def ysend(k):
        ref = wbuf.at[p]
        go(remote(ref, ref, ys.at[k - 1], yr.at[k - 1], (pop_of((yl + k) % NYL, x, core), t)))

    def ywait(k):
        ref = wbuf.at[wblock(k, 0)]
        remote(ref, ref, ys.at[k - 1], yr.at[k - 1], other_core).wait_recv()

    def csend(k, dx):
        ref = wbuf.at[wblock(k, dx)]
        i = k * NX + (dx % NX)
        go(remote(ref, ref, cs.at[i], cr.at[i], other_core))

    def cwait(k, dx):
        ref = wbuf.at[pop_of((yl + NYL - k) % NYL, (x + dx + NX) % NX, 1 - core)]
        i = k * NX + (dx % NX)
        remote(ref, ref, cs.at[i], cr.at[i], other_core).wait_recv()

    def xsend(k):
        ref = wbuf.at[wblock(k, 0)]
        go(remote(ref, ref, xs.at[0, k], xr.at[0, k], at_x(x + 1)))
        go(remote(ref, ref, xs.at[1, k], xr.at[1, k], at_x(x + NX - 1)))
        csend(k, 0)

    lo, hi = pl.ds(0, WHALF), pl.ds(WHALF, WB - WHALF)

    def xwait(k):
        for way, dx, part, dev in ((0, -1, lo, at_x(x + 1)), (1, 1, hi, at_x(x + NX - 1))):
            ref = wbuf.at[wblock(k, dx)]
            remote(ref, ref, xs.at[way, k], xr.at[way, k], other_core).wait_recv()
            ref = wbuf.at[wblock(k, dx), part]
            go(remote(ref, ref, fs.at[way, k], fr.at[way, k], dev))
            csend(k, dx)

    def fwait(k):
        for way, part in ((0, lo), (1, hi)):
            ref = wbuf.at[wblock(k, 2), part]
            remote(ref, ref, fs.at[way, k], fr.at[way, k], other_core).wait_recv()
        csend(k, 2)

    def left_copy(block, c, src_p):
        ref = tokbuf.at[block, pl.ds(ROWS, MEM), pl.ds(c * KB, KB)]
        to = 2 * block + c
        return remote(ref, leftbuf.at[src_p], las.at[to], lar.at[src_p], (to, t))

    def product(j, _):
        ring, i = j // NZ, j % NZ
        odd = i % 2
        off = (odd * ((i + 1) // 2) + (1 - odd) * (NZ - i // 2)) % NZ
        block = ((z + off) % NZ) * 2 + (yh + ring) % 2
        for c in (0, 1):
            to = 2 * block + c

            @pl.when(to != p)
            def _():
                left_copy(block, c, p).start()

            @pl.when(to == p)
            def _():
                leftbuf[p] = tokbuf[block, pl.ds(ROWS, MEM), pl.ds(c * KB, KB)]

        a = tokbuf[block, pl.ds(0, ROWS)]
        acc[...] += jnp.dot(
            a[:, :KB], wbuf[2 * block, pl.ds(0, KB)], preferred_element_type=jnp.float32
        ) + jnp.dot(a[:, KB:], wbuf[2 * block + 1, pl.ds(0, KB)], preferred_element_type=jnp.float32)
        sc[...] += lax.dot_general(
            a, tokbuf[block, pl.ds(ROWS, MEM)], (((1,), (1,)), ((), ())), preferred_element_type=jnp.float32
        )
        return 0

    def products(first, last):
        lax.fori_loop(first, last, product, 0)

    loads[0].wait()
    loads[1].wait()
    first, second = chunk(t, 0), chunk(t, 1)
    go(remote(first, relay_a, rs.at[0], rr.at[0], at_y(y + 1)))
    go(remote(second, relay_b, rs.at[1], rr.at[1], at_y(y + NY - 1)))
    for j in (0, 1):
        for way in (0, 1):
            go(zcopy(0, way, j))
    loads[2].wait()
    loads[3].wait()
    xsend(0)
    for k in (1, 3, 2):
        ysend(k)

    zevent(0, 0)
    for way, buf, c, step in ((0, relay_a, 0, 3), (1, relay_b, 1, NY - 3)):
        remote(buf, buf, rs.at[way], rr.at[way], other_core).wait_recv()
        y_to = (y + step) % NY
        y_from = (y_to + NYL) % NY
        go(remote(buf, chunk(z * 2 + y_from // NYL, c), qs.at[way], qr.at[way], at_y(y_to)))
    xwait(0)
    zevent(0, 1)
    fwait(0)
    zevent(0, 2)
    zevent(0, 3)
    for k in (1, 3):
        ywait(k)
        xsend(k)
    zevent(0, 4)
    zevent(0, 5)
    for way, c in ((0, 0), (1, 1)):
        ref = chunk(t_mate, c)
        remote(ref, ref, qs.at[way], qr.at[way], other_core).wait_recv()
    for j in (0, 1):
        for way in (0, 1):
            go(zcopy(1, way, j))
    xwait(1)
    xwait(3)
    zevent(0, 6)
    ywait(2)
    xsend(2)
    fwait(1)
    fwait(3)
    zevent(1, 0)
    xwait(2)
    zevent(1, 1)
    fwait(2)
    for k in range(NYL):
        for dx in (0, -1, 1, 2):
            cwait(k, dx)
    products(0, 4)
    zevent(1, 2)
    products(4, 8)
    zevent(1, 3)
    products(8, 11)
    zevent(1, 4)
    products(11, 13)
    zevent(1, 5)
    products(13, 15)
    loads[4].wait()
    zevent(1, 6)
    products(15, 16)

    right_rows = wbuf[p, pl.ds(KB, MEM)].astype(jnp.float32)
    lane = lax.broadcasted_iota(jnp.int32, (LEN, MEM), 1)
    place = lax.broadcasted_iota(jnp.int32, (8, 128), 0) * 128 + lax.broadcasted_iota(jnp.int32, (8, 128), 1)
    mine = jnp.zeros((8, 128), jnp.float32)
    for m in range(MEM):
        rows = pl.ds(m * LEN, LEN)
        s = jnp.sum(jnp.where(lane == m, sc[rows, :], 0.0), axis=1, keepdims=True)
        full = acc[rows, :] + (sigma_scale * s) * right_rows[m : m + 1, :] + tokbuf[t, rows].astype(jnp.float32)
        hid[rows, :] = full.astype(jnp.bfloat16)
        differ = full - tgt[rows, :].astype(jnp.float32)
        total = jnp.sum(jnp.sum(differ * differ, axis=0, keepdims=True), axis=1, keepdims=True)
        mine = mine + jnp.where(place == p * MEM + m, total, 0.0)
    loss1[t] = mine

    def tp_copy(k):
        return remote(loss1.at[t], loss1.at[t], t1s.at[k], t1r.at[k], (p, (t + k) % NTP))

    def tp_wait(k, _):
        ref = loss1.at[(t + NTP - k) % NTP]
        remote(ref, ref, t1s.at[k], t1r.at[k], other_core).wait_recv()
        return 0

    def pop_copy(k):
        return remote(loss2.at[p], loss2.at[p], t2s.at[k], t2r.at[k], ((p + k) % NPOP, t))

    def pop_wait(k, _):
        ref = loss2.at[(p + NPOP - k) % NPOP]
        remote(ref, ref, t2s.at[k], t2r.at[k], other_core).wait_recv()
        return 0

    def started(copy):
        def body(k, _):
            copy(k).start()
            return 0
        return body

    lax.fori_loop(1, NTP, started(tp_copy), 0)
    hid_out = pltpu.make_async_copy(hid, hid_hbm, loc.at[5])
    hid_out.start()

    def left_wait(k, _):
        src_p = (p + NPOP - k) % NPOP
        ref = leftbuf.at[src_p]
        remote(ref, ref, las.at[src_p], lar.at[src_p], other_core).wait_recv()
        return 0

    lax.fori_loop(1, NPOP, left_wait, 0)
    left_t[...] = leftbuf[...].reshape(MEMBERS, KB).astype(jnp.float32).T

    lax.fori_loop(1, NTP, tp_wait, 0)
    loss2[p] = jnp.sum(loss1[...], axis=0)
    lax.fori_loop(1, NPOP, started(pop_copy), 0)
    lax.fori_loop(1, NPOP, pop_wait, 0)
    losses = jnp.sum(loss2[...], axis=0) / (LEN * D)
    mean = jnp.sum(losses) / MEMBERS
    spread = jnp.sum(losses * losses) / MEMBERS - mean * mean
    fitness = -(losses - mean) / jnp.sqrt(jnp.full((8, 128), spread + epsilon, jnp.float32))

    total = None
    for q in range(4):
        part = left_t[:, q * 128 : (q + 1) * 128] * fitness[q : q + 1, :]
        r = wbuf[pl.ds(q * 8, 8), pl.ds(KB, MEM)].reshape(128, COLS)
        b1 = part.astype(jnp.bfloat16)
        rest = part - b1.astype(jnp.float32)
        b2 = rest.astype(jnp.bfloat16)
        b3 = (rest - b2.astype(jnp.float32)).astype(jnp.bfloat16)
        d = (
            jnp.dot(b3, r, preferred_element_type=jnp.float32)
            + jnp.dot(b2, r, preferred_element_type=jnp.float32)
            + jnp.dot(b1, r, preferred_element_type=jnp.float32)
        )
        total = d if total is None else total + d
    upd[...] = total * (1.0 / (MEMBERS * sigma_scale))
    upd_out = pltpu.make_async_copy(upd, upd_hbm, loc.at[6])
    upd_out.start()

    for c in sent:
        c.wait_send()

    def left_sent(k, _):
        to = (p + k) % NPOP
        ref = tokbuf.at[to // 2, pl.ds(ROWS, MEM), pl.ds(0, KB)]
        remote(ref, leftbuf.at[p], las.at[to], lar.at[p], (to, t)).wait_send()
        return 0

    def tp_sent(k, _):
        tp_copy(k).wait_send()
        return 0

    def pop_sent(k, _):
        pop_copy(k).wait_send()
        return 0

    lax.fori_loop(1, NPOP, left_sent, 0)
    lax.fori_loop(1, NTP, tp_sent, 0)
    lax.fori_loop(1, NPOP, pop_sent, 0)
    hid_out.wait()
    upd_out.wait()


def per_device(tokens, weight, left, right, target):
    dma = pltpu.SemaphoreType.DMA
    bf, f32 = jnp.bfloat16, jnp.float32
    return pl.pallas_call(
        kernel,
        out_shape=(jax.ShapeDtypeStruct((ROWS, COLS), bf), jax.ShapeDtypeStruct((KB, COLS), f32)),
        in_specs=[pl.BlockSpec(memory_space=pl.ANY)] * 5,
        out_specs=(pl.BlockSpec(memory_space=pl.ANY), pl.BlockSpec(memory_space=pl.ANY)),
        scratch_shapes=[
            pltpu.VMEM((NTP, TB, COLS), bf),
            pltpu.VMEM((NPOP, WB, COLS), bf),
            pltpu.VMEM((HALF, COLS), bf),
            pltpu.VMEM((TB - HALF, COLS), bf),
            pltpu.VMEM((ROWS, COLS), f32),
            pltpu.VMEM((ROWS, MEM), f32),
            pltpu.VMEM((ROWS, COLS), bf),
            pltpu.VMEM((ROWS, COLS), bf),
            pltpu.VMEM((NPOP, MEM, KB), bf),
            pltpu.VMEM((KB, MEMBERS), f32),
            pltpu.VMEM((KB, COLS), f32),
            pltpu.VMEM((NTP, 8, 128), f32),
            pltpu.VMEM((NPOP, 8, 128), f32),
            dma((7,)),
            dma((2, 2, 7)), dma((2, 2, 7)),
            dma((3,)), dma((3,)),
            dma((2, 4)), dma((2, 4)),
            dma((2, 4)), dma((2, 4)),
            dma((16,)), dma((16,)),
            dma((2,)), dma((2,)),
            dma((2,)), dma((2,)),
            dma((NPOP,)), dma((NPOP,)),
            dma((NTP,)), dma((NTP,)),
            dma((NPOP,)), dma((NPOP,)),
        ],
        compiler_params=pltpu.CompilerParams(
            collective_id=0, has_side_effects=True, vmem_limit_bytes=56 * 1024 * 1024
        ),
    )(tokens, weight, left, right, target)


def solution(mesh):
    return jax.shard_map(
        per_device,
        mesh=mesh,
        in_specs=(P("pop", "tp"), P("pop", "tp"), P("pop", "tp"), P("pop", "tp"), P("pop", "tp")),
        out_specs=(P("pop", "tp"), P("pop", "tp")),
        check_vma=False,
    )
```

time: 387 us -> 128 us (0.33)
  waiting for transfers between devices: 297 us -> 0 us
  Pallas kernels: 0 us -> 125 us
  blocking collectives: 22 us -> 0 us
  matrix products: 17.6 us -> 0 us
  between operations: 16.7 us -> 0.65 us
  starting transfers between devices: 14.6 us -> 0 us
  local copies, waits for them, and re-layouts: 15.6 us -> 2.72 us
    all_gather x2 -> x0, waiting for transfers between devices: 266 us -> none  [the longest x1 210 us: side_by_side(): lax.all_gather(both, axis, axis=dim, tiled=True)]
    pallas_call x0 -> x1, Pallas kernels: none -> 125 us  [per_device(): pl.pallas_call(kernel, out_shape=(jax.ShapeDtypeStruct((ROWS, COLS), bf),...]
    all_to_all x3 -> x0, waiting for transfers between devices: 29.8 us -> none  [the longest x2 23 us: copy_for_each(): lax.all_to_all(jnp.broadcast_to(x[None], (length, *x.shape)), axis, 0, 0,...]
    all_to_all x1 -> x0, blocking collectives: 22 us -> none  [copy_for_each(): lax.all_to_all(jnp.broadcast_to(x[None], (length, *x.shape)), axis, 0, 0,...]
    dot_general x3 -> x0, matrix products: 17.6 us -> none  [the longest x1 10.5 us: per_device(): base = jnp.dot(whole_tok, full_weight, preferred_element_type=jnp.float32)]
    all_to_all x3 -> x0, starting transfers between devices: 14.6 us -> none  [the longest x2 10.4 us: copy_for_each(): lax.all_to_all(jnp.broadcast_to(x[None], (length, *x.shape)), axis, 0, 0,...]
    slice x2 -> x0, local copies, waits for them, and re-layouts: 8.59 us -> none  [side_by_side(): lax.slice_in_dim(filled, at, at + a.shape[along], axis=along)]
  transfers between devices with their start and end apart: 5 -> 0, of which waited for: 5 -> 0; matrix products, arithmetic and copies ran while one was open for 5% -> 0% of each run, Pallas kernels for 0% -> 0%
where the time goes in v1:
time: 128 us
  Pallas kernels  125 us (98%)
  local copies, waits for them, and re-layouts  2.72 us (2%)
    pallas_call x1, Pallas kernels, per_device(): pl.pallas_call(kernel, out_shape=(jax.ShapeDtypeStruct((ROWS, COLS), bf),...  125 us
    unnamed x4, local copies, waits for them, and re-layouts  2.72 us

profile of v1, /device:TPU:1, one launch (start us, length us, event | category | flops | bytes accessed | tf_op | source)
XLA Modules:
  0.0 128.0 jit_solution(4019629437783293120)
XLA Ops:
  0.6 124.6 %shard_map.68 = (bf16[512,512]{1,0:T(8,128)(2,1)}, f32[256,512]{1,0:T(8,128)}) custom-call(bf16[512,512]{1,0:T(8,128)(2,1)} %tok_hbm.1, bf16[256,512]{1,0:T(8,128)(2,1)} %w_hbm.1, bf16[16,512]{1,0:T(8,128)(2,1)} %left_hbm.1, bf16[16,512]{1,0:T(8,128)(2,1)} %right_hbm.1, bf16[512,512]{1,0:T(8,128)(2,1)} %tgt_hbm.1), custom_call_target="tpu_custom_call" | custom-call | tf_op jit(solution)/shard_map/pallas_call | solution.py:359
  125.3 0.0 copy-start
  125.3 1.9 %copy.9 = bf16[512,512]{1,0:T(8,128)(2,1)} copy(bf16[512,512]{1,0:T(8,128)(2,1)} %get-tuple-element.4) | data formatting | bytes 1048576
  127.2 0.0 copy-done
  127.2 0.8 copy.10
Async XLA Ops:
  125.3 1.9 %copy-start = (f32[256,512]{1,0:T(8,128)S(1)}, f32[256,512]{1,0:T(8,128)}, u32[]{:S(2)}) copy-start(f32[256,512]{1,0:T(8,128)} %get-tuple-element.5) | copy-start | bytes 1572868

commit v2 on v0

v2 whole, which is shorter than its diff:
```python
import functools

import jax
import jax.numpy as jnp
from jax import lax
from jax.experimental import pallas as pl
from jax.experimental.pallas import tpu as pltpu
from jax.sharding import PartitionSpec as P

D = 8192
LEN = 32
MEMBERS = 512

sigma_scale = 0.5
epsilon = 1e-06

MESH = pl.DeviceIdType.MESH
NX, NY, NYL, NZ = 4, 8, 4, 8
NPOP, NTP = 32, 16
ROWS = 512
COLS = 512
KB = 256
MEM = 16
TB = ROWS + MEM
WB = KB + MEM
HALF = 256
WHALF = 128


def kernel(
    tok_hbm, w_hbm, left_hbm, right_hbm, tgt_hbm, hid, upd,
    tokbuf, wbuf, relay_a, relay_b, acc, sc, tgt, leftbuf, left_t, loss1, loss2,
    loc, z_sent, zr, t_sent, rr, mr, y_sent, w_sent, yr, xr, fr, cr, small_sent, small_got,
):
    p = lax.axis_index("pop")
    t = lax.axis_index("tp")
    core = p % 2
    x = (p // 2) % NX
    yl = p // (2 * NX)
    z = t // 2
    yh = t % 2
    y = yh * NYL + yl

    def pop_of(yl_, x_, c_):
        return (yl_ * NX + x_) * 2 + c_

    def at_yx(y_, x_):
        return (pop_of(y_ % NYL, x_, core), z * 2 + y_ // NYL)

    def at_y(y_):
        return at_yx(y_ % NY, x)

    def at_x(x_):
        return (pop_of(yl, x_ % NX, core), t)

    def at_z(z_):
        return (p, (z_ % NZ) * 2 + yh)

    other_core = (pop_of(yl, x, 1 - core), t)

    middle = (yl == 1) | (yl == 2)
    edge = jnp.logical_not(middle)

    barrier = pltpu.get_barrier_semaphore()
    near = [at_y(y + k + NY) for k in (1, -1, 3, -3)]
    near += [at_x(x + 1), at_x(x + NX - 1), at_z(z + 1), at_z(z + NZ - 1), other_core]
    for d in near:
        pl.semaphore_signal(barrier, inc=1, device_id=d, device_id_type=MESH)
    loads = [
        pltpu.make_async_copy(tok_hbm, tokbuf.at[t, pl.ds(0, ROWS)], loc.at[0]),
        pltpu.make_async_copy(left_hbm, tokbuf.at[t, pl.ds(ROWS, MEM)], loc.at[1]),
        pltpu.make_async_copy(w_hbm, wbuf.at[p, pl.ds(0, KB)], loc.at[2]),
        pltpu.make_async_copy(right_hbm, wbuf.at[p, pl.ds(KB, MEM)], loc.at[3]),
        pltpu.make_async_copy(tgt_hbm, tgt, loc.at[4]),
    ]
    for c in loads:
        c.start()

    acc[...] = jnp.zeros_like(acc)
    sc[...] = jnp.zeros_like(sc)
    pl.semaphore_wait(barrier, len(near))

    def remote(src, dst, s, r, dev):
        return pltpu.make_async_remote_copy(
            src_ref=src, dst_ref=dst, send_sem=s, recv_sem=r, device_id=dev, device_id_type=MESH
        )

    def got(ref, sem):
        remote(ref, ref, z_sent, sem, other_core).wait_recv()

    def left_device(ref, sem):
        remote(ref, ref, sem, mr.at[0], other_core).wait_send()

    def chunk(block, c):
        return tokbuf.at[block, pl.ds(0, HALF)] if c == 0 else tokbuf.at[block, pl.ds(HALF, TB - HALF)]

    def ring_chunk(ring, way, j, dist):
        c = j % 2 if way == 0 else 1 - j % 2
        src_z = z + NZ - dist if way == 0 else z + dist
        return chunk((src_z % NZ) * 2 + (yh if ring == 0 else 1 - yh), c)

    def zsend(ring, j):
        for way in (0, 1):
            zsend_way(ring, way, j)

    def zsend_way(ring, way, j):
        ref = ring_chunk(ring, way, j, j // 2)
        dev = at_z(z + 1) if way == 0 else at_z(z + NZ - 1)
        remote(ref, ref, z_sent, zr.at[way, ring, j], dev).start()

    def zevent(ring, j):
        for way in (0, 1):
            got(ring_chunk(ring, way, j, j // 2 + 1), zr.at[way, ring, j])
            if j + 2 < 7 - ring:
                zsend_way(ring, way, j + 2)

    def to_relay(n, block):
        first, second = chunk(block, 0), chunk(block, 1)
        remote(first, relay_a.at[n], t_sent, rr.at[n, 0], at_y(y + 1)).start()
        remote(second, relay_b.at[n], t_sent, rr.at[n, 1], at_y(y + NY - 1)).start()

    def from_relay(n, src_z):
        for way, buf, step in ((0, relay_a.at[n], 3), (1, relay_b.at[n], NY - 3)):
            got(buf, rr.at[n, way])
            y_to = (y + step) % NY
            y_from = (y_to + NYL) % NY
            dst = chunk((src_z % NZ) * 2 + y_from // NYL, way)
            remote(buf, dst, t_sent, mr.at[n], at_y(y_to)).start()

    def mate(n, src_z):
        got(tokbuf.at[(src_z % NZ) * 2 + (1 - yh)], mr.at[n])

    near_y = yl - 1 + 2 * ((3 - yl) // 3)
    far_y = 3 * ((3 - yl) // 2)
    group = (yl, near_y, 6 - yl - near_y - far_y, far_y)

    def wblock(k, dx):
        return wbuf.at[pop_of(group[k], (x + dx + NX) % NX, core)]

    def csend(k, dx):
        ref = wblock(k, dx)
        remote(ref, ref, w_sent, cr.at[k], other_core).start()

    def xsend(k):
        ref = wblock(k, 0)
        remote(ref, ref, w_sent, xr.at[0, k], at_x(x + 1)).start()
        remote(ref, ref, w_sent, xr.at[1, k], at_x(x + NX - 1)).start()
        csend(k, 0)

    def ysend(k, up, down):
        ref = wblock(k, 0)

        @pl.when(up)
        def _():
            remote(ref, ref, y_sent, yr.at[group[k]], (pop_of((yl + 1) % NYL, x, core), t)).start()

        @pl.when(down)
        def _():
            remote(ref, ref, y_sent, yr.at[group[k]], (pop_of((yl + NYL - 1) % NYL, x, core), t)).start()

    def yown():
        ysend(0, yl < NYL - 1, yl > 0)

    def ywait(k):
        src = group[k]
        got(wblock(k, 0), yr.at[src])
        ysend(k, (src < yl) & (yl < NYL - 1), (src > yl) & (yl > 0))
        xsend(k)

    lo, hi = pl.ds(0, WHALF), pl.ds(WHALF, WB - WHALF)

    def xwait(k):
        for way, dx, part, dev in ((0, -1, lo, at_x(x + 1)), (1, 1, hi, at_x(x + NX - 1))):
            got(wblock(k, dx), xr.at[way, k])
            ref = wblock(k, dx).at[part]
            remote(ref, ref, w_sent, fr.at[k], dev).start()
            csend(k, dx)

    def fwait(k):
        got(wblock(k, 2), fr.at[k])
        csend(k, 2)

    def base_rows(block, rows):
        a = tokbuf[block, rows]
        acc[rows, :] += jnp.dot(
            a[:, :KB], wbuf[2 * block, pl.ds(0, KB)], preferred_element_type=jnp.float32
        ) + jnp.dot(a[:, KB:], wbuf[2 * block + 1, pl.ds(0, KB)], preferred_element_type=jnp.float32)

    def score_rows(block, rows):
        sc[rows, :] += lax.dot_general(
            tokbuf[block, rows], tokbuf[block, pl.ds(ROWS, MEM)], (((1,), (1,)), ((), ())),
            preferred_element_type=jnp.float32,
        )

    def left_rows(block):
        for c in (0, 1):
            to = 2 * block + c
            ref = tokbuf.at[block, pl.ds(ROWS, MEM), pl.ds(c * KB, KB)]

            @pl.when(to != p)
            def _():
                remote(ref, leftbuf.at[p], small_sent.at[0], small_got.at[0], (to, t)).start()

            @pl.when(to == p)
            def _():
                leftbuf[p] = ref[...]

    every = pl.ds(0, ROWS)

    def product(block):
        left_rows(block)
        base_rows(block, every)
        score_rows(block, every)

    def at_offset(ring, off):
        return ((z + off) % NZ) * 2 + (yh + ring) % 2

    def group_products(k):
        got(wbuf.at[pl.ds(0, NX)], cr.at[k])

        def body(i, _):
            product((group[k] * 2 + i) * 2 + yh)
            return 0

        lax.fori_loop(0, 2, body, 0)

    def ring_products(first, last):
        def body(i, _):
            odd = i % 2
            product(at_offset(1, (odd * ((i + 1) // 2) + (1 - odd) * (NZ - i // 2)) % NZ))
            return 0

        lax.fori_loop(first, last, body, 0)

    top, low = pl.ds(0, HALF), pl.ds(HALF, ROWS - HALF)

    loads[0].wait()
    loads[1].wait()
    zsend(0, 0)
    zsend(0, 1)
    loads[2].wait()
    loads[3].wait()
    yown()
    to_relay(0, t)
    xsend(0)

    middle = (yl == 1) | (yl == 2)
    edge = jnp.logical_not(middle)

    zevent(0, 0)
    ywait(1)
    pl.when(middle)(functools.partial(ywait, 2))
    xwait(0)
    zevent(0, 1)
    from_relay(0, z)
    zevent(0, 2)
    pl.when(middle)(functools.partial(ywait, 3))
    pl.when(edge)(functools.partial(ywait, 2))
    zevent(0, 3)
    xwait(1)
    fwait(0)
    zevent(0, 4)
    zevent(0, 5)
    mate(0, z)
    zsend(1, 0)
    zsend(1, 1)
    xwait(2)
    zevent(0, 6)
    to_relay(1, at_offset(0, 4))
    pl.when(edge)(functools.partial(ywait, 3))
    fwait(1)
    zevent(1, 0)
    fwait(2)
    group_products(0)
    zevent(1, 1)
    from_relay(1, z + 4)
    xwait(3)
    group_products(1)
    zevent(1, 2)
    group_products(2)
    fwait(3)
    zevent(1, 3)
    group_products(3)
    ring_products(0, 3)
    zevent(1, 4)
    ring_products(3, 5)
    before, after = at_offset(1, NZ - 3), at_offset(1, 3)
    base_rows(before, top)
    base_rows(after, low)
    score_rows(after, low)
    loads[4].wait()
    mate(1, z + 4)
    product(at_offset(1, 4))
    zevent(1, 5)
    base_rows(before, low)
    base_rows(after, top)
    score_rows(before, every)
    score_rows(after, top)
    left_rows(before)
    left_rows(after)

    right_rows = wbuf[p, pl.ds(KB, MEM)].astype(jnp.float32)
    lane = lax.broadcasted_iota(jnp.int32, (LEN, MEM), 1)
    place = lax.broadcasted_iota(jnp.int32, (1, 128), 1)
    mine = jnp.zeros((1, 128), jnp.float32)
    for m in range(MEM):
        rows = pl.ds(m * LEN, LEN)
        s = jnp.sum(jnp.where(lane == m, sc[rows, :], 0.0), axis=1, keepdims=True)
        full = acc[rows, :] + (sigma_scale * s) * right_rows[m : m + 1, :] + tokbuf[t, rows].astype(jnp.float32)
        hid[rows, :] = full.astype(jnp.bfloat16)
        differ = full - tgt[rows, :].astype(jnp.float32)
        total = jnp.sum(jnp.sum(differ * differ, axis=0, keepdims=True), axis=1, keepdims=True)
        mine = mine + jnp.where(place == (p % 8) * MEM + m, total, 0.0)
    loss1[z * 2 + core] = mine

    ref = loss1.at[z * 2 + core]
    for dz in (4, 3, 5, 2, 6, 1, 7, 0):
        for dc in (1, 0):
            if dz or dc:
                dev = (pop_of(yl, x, (core + dc) % 2), ((z + dz) % NZ) * 2 + yh)
                remote(ref, ref, small_sent.at[1], small_got.at[1], dev).start()

    got(leftbuf.at[pl.ds(0, NPOP - 1)], small_got.at[0])
    left_t[...] = leftbuf[...].reshape(MEMBERS, KB).astype(jnp.float32).T

    got(loss1.at[pl.ds(0, 15)], small_got.at[1])
    row = loss1[0]
    for i in range(1, 16):
        row = row + loss1[i]
    loss2[y * NX + x] = row
    ref = loss2.at[y * NX + x]
    for dy in (4, 3, 5, 2, 6, 1, 7, 0):
        for dx in (2, 1, 3, 0):
            if dy or dx:
                remote(ref, ref, small_sent.at[2], small_got.at[2], at_yx((y + dy) % NY, (x + dx) % NX)).start()
    got(loss2.at[pl.ds(0, 31)], small_got.at[2])

    losses = []
    for q in range(NYL):
        row = loss2[q * NX]
        for i in range(1, NX):
            row = row + loss2[q * NX + i]
        for i in range(NX):
            row = row + loss2[(NYL + q) * NX + i]
        losses.append(row / (LEN * D))
    mean = jnp.sum(losses[0] + losses[1] + losses[2] + losses[3]) / MEMBERS
    squares = [row * row for row in losses]
    spread = jnp.sum(squares[0] + squares[1] + squares[2] + squares[3]) / MEMBERS - mean * mean
    root = jnp.sqrt(jnp.full((1, 128), spread + epsilon, jnp.float32))

    fitness = jnp.concatenate([-(row - mean) / root for row in losses], axis=1)
    weighted = left_t[...] * fitness
    b1 = weighted.astype(jnp.bfloat16)
    b2 = (weighted - b1.astype(jnp.float32)).astype(jnp.bfloat16)
    r = wbuf[:, pl.ds(KB, MEM)].reshape(MEMBERS, COLS)
    total = jnp.dot(b2, r, preferred_element_type=jnp.float32) + jnp.dot(b1, r, preferred_element_type=jnp.float32)
    upd[...] = total * (1.0 / (MEMBERS * sigma_scale))

    left_device(tokbuf.at[pl.ds(0, 13)], z_sent)
    left_device(tokbuf.at[pl.ds(0, 4)], t_sent)
    left_device(wbuf.at[pl.ds(0, 28)], w_sent)
    @pl.when(middle)
    def _():
        left_device(wbuf.at[pl.ds(0, 5)], y_sent)

    @pl.when(edge)
    def _():
        left_device(wbuf.at[0], y_sent)

    left_device(leftbuf.at[pl.ds(0, NPOP - 1)], small_sent.at[0])
    left_device(loss1.at[pl.ds(0, 15)], small_sent.at[1])
    left_device(loss2.at[pl.ds(0, 31)], small_sent.at[2])


def write_out(hid, upd, hid_hbm, upd_hbm, sem):
    copies = [pltpu.make_async_copy(hid, hid_hbm, sem.at[0]), pltpu.make_async_copy(upd, upd_hbm, sem.at[1])]
    for c in copies:
        c.start()
    for c in copies:
        c.wait()


def per_device(tokens, weight, left, right, target):
    dma = pltpu.SemaphoreType.DMA
    bf, f32 = jnp.bfloat16, jnp.float32
    hidden, update = pl.pallas_call(
        kernel,
        out_shape=(pltpu.VMEM((ROWS, COLS), bf), pltpu.VMEM((KB, COLS), f32)),
        in_specs=[pl.BlockSpec(memory_space=pl.ANY)] * 5,
        out_specs=(pl.BlockSpec(memory_space=pltpu.VMEM), pl.BlockSpec(memory_space=pltpu.VMEM)),
        scratch_shapes=[
            pltpu.VMEM((NTP, TB, COLS), bf),
            pltpu.VMEM((NPOP, WB, COLS), bf),
            pltpu.VMEM((2, HALF, COLS), bf),
            pltpu.VMEM((2, TB - HALF, COLS), bf),
            pltpu.VMEM((ROWS, COLS), f32),
            pltpu.VMEM((ROWS, MEM), f32),
            pltpu.VMEM((ROWS, COLS), bf),
            pltpu.VMEM((NPOP, MEM, KB), bf),
            pltpu.VMEM((KB, MEMBERS), f32),
            pltpu.VMEM((16, 1, 128), f32),
            pltpu.VMEM((32, 1, 128), f32),
            dma((5,)),
            dma(()), dma((2, 2, 7)),
            dma(()), dma((2, 2)), dma((2,)),
            dma(()), dma(()), dma((NYL,)), dma((2, 4)), dma((4,)), dma((4,)),
            dma((3,)), dma((3,)),
        ],
        compiler_params=pltpu.CompilerParams(
            collective_id=0, has_side_effects=True, vmem_limit_bytes=56 * 1024 * 1024
        ),
    )(tokens, weight, left, right, target)
    return pl.pallas_call(
        write_out,
        out_shape=(jax.ShapeDtypeStruct((ROWS, COLS), bf), jax.ShapeDtypeStruct((KB, COLS), f32)),
        in_specs=[pl.BlockSpec(memory_space=pl.ANY)] * 2,
        out_specs=(pl.BlockSpec(memory_space=pl.ANY), pl.BlockSpec(memory_space=pl.ANY)),
        scratch_shapes=[dma((2,))],
        compiler_params=pltpu.CompilerParams(vmem_limit_bytes=1024 * 1024),
    )(hidden, update)


def solution(mesh):
    return jax.shard_map(
        per_device,
        mesh=mesh,
        in_specs=(P("pop", "tp"), P("pop", "tp"), P("pop", "tp"), P("pop", "tp"), P("pop", "tp")),
        out_specs=(P("pop", "tp"), P("pop", "tp")),
        check_vma=False,
    )
```

time: 387 us -> 105 us (0.27)
  waiting for transfers between devices: 297 us -> 0 us
  Pallas kernels: 0 us -> 104 us
  blocking collectives: 22 us -> 0 us
  matrix products: 17.6 us -> 0 us
  between operations: 16.7 us -> 0.64 us
  local copies, waits for them, and re-layouts: 15.6 us -> 0 us
  starting transfers between devices: 14.6 us -> 0 us
    all_gather x2 -> x0, waiting for transfers between devices: 266 us -> none  [the longest x1 210 us: side_by_side(): lax.all_gather(both, axis, axis=dim, tiled=True)]
    pallas_call x0 -> x2, Pallas kernels: none -> 104 us  [the longest x1 103 us: per_device(): pl.pallas_call(kernel, out_shape=(pltpu.VMEM((ROWS, COLS), bf), pltpu.VME...]
    all_to_all x3 -> x0, waiting for transfers between devices: 29.8 us -> none  [the longest x2 23 us: copy_for_each(): lax.all_to_all(jnp.broadcast_to(x[None], (length, *x.shape)), axis, 0, 0,...]
    all_to_all x1 -> x0, blocking collectives: 22 us -> none  [copy_for_each(): lax.all_to_all(jnp.broadcast_to(x[None], (length, *x.shape)), axis, 0, 0,...]
    dot_general x3 -> x0, matrix products: 17.6 us -> none  [the longest x1 10.5 us: per_device(): base = jnp.dot(whole_tok, full_weight, preferred_element_type=jnp.float32)]
    all_to_all x3 -> x0, starting transfers between devices: 14.6 us -> none  [the longest x2 10.4 us: copy_for_each(): lax.all_to_all(jnp.broadcast_to(x[None], (length, *x.shape)), axis, 0, 0,...]
    slice x2 -> x0, local copies, waits for them, and re-layouts: 8.59 us -> none  [side_by_side(): lax.slice_in_dim(filled, at, at + a.shape[along], axis=along)]
  transfers between devices with their start and end apart: 5 -> 0, of which waited for: 5 -> 0; matrix products, arithmetic and copies ran while one was open for 5% -> 0% of each run, Pallas kernels for 0% -> 0%
where the time goes in v2:
time: 105 us
  Pallas kernels  104 us (99%)
    pallas_call x1, Pallas kernels, per_device(): pl.pallas_call(kernel, out_shape=(pltpu.VMEM((ROWS, COLS), bf), pltpu.VME...  103 us

profile of v2, /device:TPU:1, one launch (start us, length us, event | category | flops | bytes accessed | tf_op | source)
XLA Modules:
  0.0 104.9 jit_solution(9216031942117592268)
XLA Ops:
  0.6 103.3 %shard_map.68 = (bf16[512,512]{1,0:T(8,128)(2,1)S(1)}, f32[256,512]{1,0:T(8,128)S(1)}) custom-call(bf16[512,512]{1,0:T(8,128)(2,1)} %tok_hbm.1, bf16[256,512]{1,0:T(8,128)(2,1)} %w_hbm.1, bf16[16,512]{1,0:T(8,128)(2,1)} %left_hbm.1, bf16[16,512]{1,0:T(8,128)(2,1)} %right_hbm.1, bf16[512,512]{1,0:T(8,128)(2,1)} %tgt_hbm.1), custom_call_target="tpu_custom_call" | custom-call | tf_op jit(solution)/shard_map/pallas_call | solution.py:386
  103.9 1.0 shard_map.69

commit v3 on v2

--- a/solution.py
+++ b/solution.py
@@ -23,6 +23,8 @@
 MEM = 16
 TB = ROWS + MEM
 WB = KB + MEM
+QUARTER = 128
+EXTRA = 32
 HALF = 256
 WHALF = 128
 
@@ -31,6 +33,7 @@
     tok_hbm, w_hbm, left_hbm, right_hbm, tgt_hbm, hid, upd,
     tokbuf, wbuf, relay_a, relay_b, acc, sc, tgt, leftbuf, left_t, loss1, loss2,
     loc, z_sent, zr, t_sent, rr, mr, y_sent, w_sent, yr, xr, fr, cr, small_sent, small_got,
+    entered,
 ):
     p = lax.axis_index("pop")
     t = lax.axis_index("tp")
@@ -62,7 +65,7 @@
     edge = jnp.logical_not(middle)
 
     barrier = pltpu.get_barrier_semaphore()
-    near = [at_y(y + k + NY) for k in (1, -1, 3, -3)]
+    near = [at_y(y + 1), at_y(y + NY - 1)]
     near += [at_x(x + 1), at_x(x + NX - 1), at_z(z + 1), at_z(z + NZ - 1), other_core]
     for d in near:
         pl.semaphore_signal(barrier, inc=1, device_id=d, device_id_type=MESH)
@@ -86,7 +89,7 @@
         )
 
     def got(ref, sem):
-        remote(ref, ref, z_sent, sem, other_core).wait_recv()
+        remote(ref, ref, z_sent.at[0], sem, other_core).wait_recv()
 
     def left_device(ref, sem):
         remote(ref, ref, sem, mr.at[0], other_core).wait_send()
@@ -97,38 +100,67 @@
     def ring_chunk(ring, way, j, dist):
         c = j % 2 if way == 0 else 1 - j % 2
         src_z = z + NZ - dist if way == 0 else z + dist
-        return chunk((src_z % NZ) * 2 + (yh if ring == 0 else 1 - yh), c)
+        block = (src_z % NZ) * 2 + (yh if ring == 0 else 1 - yh)
+        if ring == 1 and j >= 5:
+            c = 1 - way
+            rows = QUARTER if j == 6 else QUARTER - EXTRA
+            return tokbuf.at[block, pl.ds(c * HALF + (6 - j) * QUARTER, rows)]
+        return chunk(block, c)
 
     def zsend(ring, j):
         for way in (0, 1):
             zsend_way(ring, way, j)
 
     def zsend_way(ring, way, j):
-        ref = ring_chunk(ring, way, j, j // 2)
+        ref = ring_chunk(ring, way, j, min(j // 2, 2 if ring == 1 else 3))
         dev = at_z(z + 1) if way == 0 else at_z(z + NZ - 1)
-        remote(ref, ref, z_sent, zr.at[way, ring, j], dev).start()
+        small = ring == 1 and j >= 5
+        remote(ref, ref, z_sent.at[1 if small else 0], zr.at[way, ring, j], dev).start()
 
     def zevent(ring, j):
         for way in (0, 1):
-            got(ring_chunk(ring, way, j, j // 2 + 1), zr.at[way, ring, j])
+            got(ring_chunk(ring, way, j, min(j // 2, 2 if ring == 1 else 3) + 1), zr.at[way, ring, j])
             if j + 2 < 7 - ring:
                 zsend_way(ring, way, j + 2)
-
-    def to_relay(n, block):
-        first, second = chunk(block, 0), chunk(block, 1)
-        remote(first, relay_a.at[n], t_sent, rr.at[n, 0], at_y(y + 1)).start()
-        remote(second, relay_b.at[n], t_sent, rr.at[n, 1], at_y(y + NY - 1)).start()
+            if ring == 1 and j == 3:
+                zsend_way(1, way, 6)
+
+    def pieces(n, own_yh, src_z):
+        if n < 2:
+            block = (src_z % NZ) * 2 + own_yh
+            return chunk(block, 0), chunk(block, 1)
+        after, before = ((z + 3) % NZ) * 2 + own_yh, ((z + NZ - 3) % NZ) * 2 + own_yh
+        return tokbuf.at[after, pl.ds(HALF - EXTRA, EXTRA)], tokbuf.at[before, pl.ds(ROWS - EXTRA, EXTRA + MEM)]
+
+    def relay(n):
+        if n < 2:
+            return relay_a.at[n], relay_b.at[n]
+        return relay_a.at[n, pl.ds(0, EXTRA)], relay_b.at[n, pl.ds(0, EXTRA + MEM)]
+
+    def to_relay(n, src_z):
+        for way, ref, buf, dev in zip((0, 1), pieces(n, yh, src_z), relay(n), (at_y(y + 1), at_y(y + NY - 1))):
+            remote(ref, buf, t_sent.at[n // 2], rr.at[n, way], dev).start()
 
     def from_relay(n, src_z):
-        for way, buf, step in ((0, relay_a.at[n], 3), (1, relay_b.at[n], NY - 3)):
+        for way, buf, step in zip((0, 1), relay(n), (3, NY - 3)):
             got(buf, rr.at[n, way])
             y_to = (y + step) % NY
-            y_from = (y_to + NYL) % NY
-            dst = chunk((src_z % NZ) * 2 + y_from // NYL, way)
-            remote(buf, dst, t_sent, mr.at[n], at_y(y_to)).start()
+            dst = pieces(n, (y_to + NYL) % NY // NYL, src_z)[way]
+            remote(buf, dst, t_sent.at[n // 2], mr.at[n], at_y(y_to)).start()
 
     def mate(n, src_z):
-        got(tokbuf.at[(src_z % NZ) * 2 + (1 - yh)], mr.at[n])
+        if n < 2:
+            got(tokbuf.at[(src_z % NZ) * 2 + (1 - yh)], mr.at[n])
+        else:
+            got(tokbuf.at[0, pl.ds(0, 2 * EXTRA + MEM)], mr.at[n])
+
+    def tell(n):
+        for way, dev in ((0, at_y(y + 1)), (1, at_y(y + NY - 1))):
+            pl.semaphore_signal(entered.at[n, way], inc=1, device_id=dev, device_id_type=MESH)
+
+    def told(n):
+        for way in (0, 1):
+            pl.semaphore_wait(entered.at[n, way], 1)
 
     near_y = yl - 1 + 2 * ((3 - yl) // 3)
     far_y = 3 * ((3 - yl) // 2)
@@ -238,25 +270,26 @@
     loads[1].wait()
     zsend(0, 0)
     zsend(0, 1)
+    tell(0)
     loads[2].wait()
     loads[3].wait()
     yown()
-    to_relay(0, t)
+    to_relay(0, z)
     xsend(0)
-
-    middle = (yl == 1) | (yl == 2)
-    edge = jnp.logical_not(middle)
+    told(0)
+    tell(1)
 
     zevent(0, 0)
     ywait(1)
     pl.when(middle)(functools.partial(ywait, 2))
     xwait(0)
     zevent(0, 1)
+    told(1)
     from_relay(0, z)
     zevent(0, 2)
+    zevent(0, 3)
     pl.when(middle)(functools.partial(ywait, 3))
     pl.when(edge)(functools.partial(ywait, 2))
-    zevent(0, 3)
     xwait(1)
     fwait(0)
     zevent(0, 4)
@@ -266,14 +299,16 @@
     zsend(1, 1)
     xwait(2)
     zevent(0, 6)
-    to_relay(1, at_offset(0, 4))
+    to_relay(1, z + 4)
+    to_relay(2, z)
     pl.when(edge)(functools.partial(ywait, 3))
     fwait(1)
     zevent(1, 0)
     fwait(2)
     group_products(0)
+    from_relay(1, z + 4)
     zevent(1, 1)
-    from_relay(1, z + 4)
+    from_relay(2, z)
     xwait(3)
     group_products(1)
     zevent(1, 2)
@@ -291,27 +326,36 @@
     loads[4].wait()
     mate(1, z + 4)
     product(at_offset(1, 4))
-    zevent(1, 5)
-    base_rows(before, low)
-    base_rows(after, top)
-    score_rows(before, every)
-    score_rows(after, top)
-    left_rows(before)
-    left_rows(after)
-
+    q0, q1, q2, q3 = (pl.ds(i * QUARTER, QUARTER) for i in range(4))
     right_rows = wbuf[p, pl.ds(KB, MEM)].astype(jnp.float32)
     lane = lax.broadcasted_iota(jnp.int32, (LEN, MEM), 1)
     place = lax.broadcasted_iota(jnp.int32, (1, 128), 1)
-    mine = jnp.zeros((1, 128), jnp.float32)
-    for m in range(MEM):
-        rows = pl.ds(m * LEN, LEN)
-        s = jnp.sum(jnp.where(lane == m, sc[rows, :], 0.0), axis=1, keepdims=True)
-        full = acc[rows, :] + (sigma_scale * s) * right_rows[m : m + 1, :] + tokbuf[t, rows].astype(jnp.float32)
-        hid[rows, :] = full.astype(jnp.bfloat16)
-        differ = full - tgt[rows, :].astype(jnp.float32)
-        total = jnp.sum(jnp.sum(differ * differ, axis=0, keepdims=True), axis=1, keepdims=True)
-        mine = mine + jnp.where(place == (p % 8) * MEM + m, total, 0.0)
-    loss1[z * 2 + core] = mine
+
+    def finish(members, mine):
+        for m in members:
+            rows = pl.ds(m * LEN, LEN)
+            s = jnp.sum(jnp.where(lane == m, sc[rows, :], 0.0), axis=1, keepdims=True)
+            full = acc[rows, :] + (sigma_scale * s) * right_rows[m : m + 1, :] + tokbuf[t, rows].astype(jnp.float32)
+            hid[rows, :] = full.astype(jnp.bfloat16)
+            differ = full - tgt[rows, :].astype(jnp.float32)
+            total = jnp.sum(jnp.sum(differ * differ, axis=0, keepdims=True), axis=1, keepdims=True)
+            mine = mine + jnp.where(place == (p % 8) * MEM + m, total, 0.0)
+        return mine
+
+    mate(2, z)
+    zevent(1, 5)
+    for block, seen, scored in ((before, q3, (top, q3)), (after, q1, (q1,))):
+        base_rows(block, seen)
+        for rows in scored:
+            score_rows(block, rows)
+        left_rows(block)
+    per = QUARTER // LEN
+    mine = finish((*range(per, 2 * per), *range(3 * per, 4 * per)), jnp.zeros((1, 128), jnp.float32))
+    zevent(1, 6)
+    for block, seen in ((before, q2), (after, q0)):
+        base_rows(block, seen)
+        score_rows(block, seen)
+    loss1[z * 2 + core] = finish((*range(per), *range(2 * per, 3 * per)), mine)
 
     ref = loss1.at[z * 2 + core]
     for dz in (4, 3, 5, 2, 6, 1, 7, 0):
@@ -356,8 +400,10 @@
     total = jnp.dot(b2, r, preferred_element_type=jnp.float32) + jnp.dot(b1, r, preferred_element_type=jnp.float32)
     upd[...] = total * (1.0 / (MEMBERS * sigma_scale))
 
-    left_device(tokbuf.at[pl.ds(0, 13)], z_sent)
-    left_device(tokbuf.at[pl.ds(0, 4)], t_sent)
+    left_device(tokbuf.at[pl.ds(0, 12)], z_sent.at[0])
+    left_device(tokbuf.at[0, pl.ds(0, 4 * QUARTER - 2 * EXTRA)], z_sent.at[1])
+    left_device(tokbuf.at[pl.ds(0, 4)], t_sent.at[0])
+    left_device(tokbuf.at[0, pl.ds(0, 2 * (2 * EXTRA + MEM))], t_sent.at[1])
     left_device(wbuf.at[pl.ds(0, 28)], w_sent)
     @pl.when(middle)
     def _():
@@ -391,8 +437,8 @@
         scratch_shapes=[
             pltpu.VMEM((NTP, TB, COLS), bf),
             pltpu.VMEM((NPOP, WB, COLS), bf),
-            pltpu.VMEM((2, HALF, COLS), bf),
-            pltpu.VMEM((2, TB - HALF, COLS), bf),
+            pltpu.VMEM((3, HALF, COLS), bf),
+            pltpu.VMEM((3, TB - HALF, COLS), bf),
             pltpu.VMEM((ROWS, COLS), f32),
             pltpu.VMEM((ROWS, MEM), f32),
             pltpu.VMEM((ROWS, COLS), bf),
@@ -401,10 +447,11 @@
             pltpu.VMEM((16, 1, 128), f32),
             pltpu.VMEM((32, 1, 128), f32),
             dma((5,)),
-            dma(()), dma((2, 2, 7)),
-            dma(()), dma((2, 2)), dma((2,)),
+            dma((2,)), dma((2, 2, 7)),
+            dma((2,)), dma((3, 2)), dma((3,)),
             dma(()), dma(()), dma((NYL,)), dma((2, 4)), dma((4,)), dma((4,)),
             dma((3,)), dma((3,)),
+            pltpu.SemaphoreType.REGULAR((2, 2)),
         ],
         compiler_params=pltpu.CompilerParams(
             collective_id=0, has_side_effects=True, vmem_limit_bytes=56 * 1024 * 1024

time: 105 us -> 103 us (0.981)
    pallas_call x1, Pallas kernels: 103 us -> 102 us  [per_device(): pl.pallas_call(kernel, out_shape=(pltpu.VMEM((ROWS, COLS), bf), pltpu.VME...]
where the time goes in v3:
time: 103 us
  Pallas kernels  103 us (100%)
    pallas_call x1, Pallas kernels, per_device(): pl.pallas_call(kernel, out_shape=(pltpu.VMEM((ROWS, COLS), bf), pltpu.VME...  102 us

profile of v3, /device:TPU:1, one launch (start us, length us, event | category | flops | bytes accessed | tf_op | source)
XLA Modules:
  0.0 103.2 jit_solution(7496812321889376525)
XLA Ops:
  0.6 101.5 %shard_map.68 = (bf16[512,512]{1,0:T(8,128)(2,1)S(1)}, f32[256,512]{1,0:T(8,128)S(1)}) custom-call(bf16[512,512]{1,0:T(8,128)(2,1)} %tok_hbm.1, bf16[256,512]{1,0:T(8,128)(2,1)} %w_hbm.1, bf16[16,512]{1,0:T(8,128)(2,1)} %left_hbm.1, bf16[16,512]{1,0:T(8,128)(2,1)} %right_hbm.1, bf16[512,512]{1,0:T(8,128)(2,1)} %tgt_hbm.1), custom_call_target="tpu_custom_call" | custom-call | tf_op jit(solution)/shard_map/pallas_call | solution.py:432
  102.2 1.0 shard_map.69

commit v4 on v3

--- a/solution.py
+++ b/solution.py
@@ -23,7 +23,7 @@
 MEM = 16
 TB = ROWS + MEM
 WB = KB + MEM
-QUARTER = 128
+LAST = 64
 EXTRA = 32
 HALF = 256
 WHALF = 128
@@ -32,7 +32,7 @@
 def kernel(
     tok_hbm, w_hbm, left_hbm, right_hbm, tgt_hbm, hid, upd,
     tokbuf, wbuf, relay_a, relay_b, acc, sc, tgt, leftbuf, left_t, loss1, loss2,
-    loc, z_sent, zr, t_sent, rr, mr, y_sent, w_sent, yr, xr, fr, cr, small_sent, small_got,
+    loc, z_sent, zr, rr, mr, y_sent, w_sent, yr, xr, fr, cr, small_sent, small_got,
     entered,
 ):
     p = lax.axis_index("pop")
@@ -65,8 +65,7 @@
     edge = jnp.logical_not(middle)
 
     barrier = pltpu.get_barrier_semaphore()
-    near = [at_y(y + 1), at_y(y + NY - 1)]
-    near += [at_x(x + 1), at_x(x + NX - 1), at_z(z + 1), at_z(z + NZ - 1), other_core]
+    near = [at_z(z + 1), at_z(z + NZ - 1), at_y(y + 1), at_y(y + NY - 1), at_x(x + 1), at_x(x + NX - 1), other_core]
     for d in near:
         pl.semaphore_signal(barrier, inc=1, device_id=d, device_id_type=MESH)
     loads = [
@@ -103,8 +102,8 @@
         block = (src_z % NZ) * 2 + (yh if ring == 0 else 1 - yh)
         if ring == 1 and j >= 5:
             c = 1 - way
-            rows = QUARTER if j == 6 else QUARTER - EXTRA
-            return tokbuf.at[block, pl.ds(c * HALF + (6 - j) * QUARTER, rows)]
+            start, rows = (0, LAST) if j == 6 else (LAST, HALF - EXTRA - LAST)
+            return tokbuf.at[block, pl.ds(c * HALF + start, rows)]
         return chunk(block, c)
 
     def zsend(ring, j):
@@ -139,14 +138,14 @@
 
     def to_relay(n, src_z):
         for way, ref, buf, dev in zip((0, 1), pieces(n, yh, src_z), relay(n), (at_y(y + 1), at_y(y + NY - 1))):
-            remote(ref, buf, t_sent.at[n // 2], rr.at[n, way], dev).start()
+            remote(ref, buf, z_sent.at[n // 2], rr.at[n], dev).start()
 
     def from_relay(n, src_z):
+        got(tokbuf.at[0] if n < 2 else tokbuf.at[0, pl.ds(0, 2 * EXTRA + MEM)], rr.at[n])
         for way, buf, step in zip((0, 1), relay(n), (3, NY - 3)):
-            got(buf, rr.at[n, way])
             y_to = (y + step) % NY
             dst = pieces(n, (y_to + NYL) % NY // NYL, src_z)[way]
-            remote(buf, dst, t_sent.at[n // 2], mr.at[n], at_y(y_to)).start()
+            remote(buf, dst, z_sent.at[n // 2], mr.at[n], at_y(y_to)).start()
 
     def mate(n, src_z):
         if n < 2:
@@ -155,12 +154,11 @@
             got(tokbuf.at[0, pl.ds(0, 2 * EXTRA + MEM)], mr.at[n])
 
     def tell(n):
-        for way, dev in ((0, at_y(y + 1)), (1, at_y(y + NY - 1))):
-            pl.semaphore_signal(entered.at[n, way], inc=1, device_id=dev, device_id_type=MESH)
+        for dev in (at_y(y + 1), at_y(y + NY - 1)):
+            pl.semaphore_signal(entered.at[n], inc=1, device_id=dev, device_id_type=MESH)
 
     def told(n):
-        for way in (0, 1):
-            pl.semaphore_wait(entered.at[n, way], 1)
+        pl.semaphore_wait(entered.at[n], 2)
 
     near_y = yl - 1 + 2 * ((3 - yl) // 3)
     far_y = 3 * ((3 - yl) // 2)
@@ -175,8 +173,8 @@
 
     def xsend(k):
         ref = wblock(k, 0)
-        remote(ref, ref, w_sent, xr.at[0, k], at_x(x + 1)).start()
-        remote(ref, ref, w_sent, xr.at[1, k], at_x(x + NX - 1)).start()
+        remote(ref, ref, w_sent, xr.at[k], at_x(x + 1)).start()
+        remote(ref, ref, w_sent, xr.at[k], at_x(x + NX - 1)).start()
         csend(k, 0)
 
     def ysend(k, up, down):
@@ -202,8 +200,8 @@
     lo, hi = pl.ds(0, WHALF), pl.ds(WHALF, WB - WHALF)
 
     def xwait(k):
-        for way, dx, part, dev in ((0, -1, lo, at_x(x + 1)), (1, 1, hi, at_x(x + NX - 1))):
-            got(wblock(k, dx), xr.at[way, k])
+        got(wbuf.at[pl.ds(0, 2)], xr.at[k])
+        for dx, part, dev in ((-1, lo, at_x(x + 1)), (1, hi, at_x(x + NX - 1))):
             ref = wblock(k, dx).at[part]
             remote(ref, ref, w_sent, fr.at[k], dev).start()
             csend(k, dx)
@@ -316,9 +314,8 @@
     fwait(3)
     zevent(1, 3)
     group_products(3)
-    ring_products(0, 3)
+    ring_products(0, 5)
     zevent(1, 4)
-    ring_products(3, 5)
     before, after = at_offset(1, NZ - 3), at_offset(1, 3)
     base_rows(before, top)
     base_rows(after, low)
@@ -326,7 +323,8 @@
     loads[4].wait()
     mate(1, z + 4)
     product(at_offset(1, 4))
-    q0, q1, q2, q3 = (pl.ds(i * QUARTER, QUARTER) for i in range(4))
+    firsts = pl.ds(0, LAST), pl.ds(HALF, LAST)
+    rests = pl.ds(LAST, HALF - LAST), pl.ds(HALF + LAST, ROWS - HALF - LAST)
     right_rows = wbuf[p, pl.ds(KB, MEM)].astype(jnp.float32)
     lane = lax.broadcasted_iota(jnp.int32, (LEN, MEM), 1)
     place = lax.broadcasted_iota(jnp.int32, (1, 128), 1)
@@ -344,18 +342,18 @@
 
     mate(2, z)
     zevent(1, 5)
-    for block, seen, scored in ((before, q3, (top, q3)), (after, q1, (q1,))):
+    for block, seen, scored in ((before, rests[1], (top, rests[1])), (after, rests[0], (rests[0],))):
         base_rows(block, seen)
         for rows in scored:
             score_rows(block, rows)
         left_rows(block)
-    per = QUARTER // LEN
-    mine = finish((*range(per, 2 * per), *range(3 * per, 4 * per)), jnp.zeros((1, 128), jnp.float32))
+    last_members = [m for m in range(MEM) if m * LEN % HALF < LAST]
+    mine = finish([m for m in range(MEM) if m not in last_members], jnp.zeros((1, 128), jnp.float32))
     zevent(1, 6)
-    for block, seen in ((before, q2), (after, q0)):
+    for block, seen in ((before, firsts[1]), (after, firsts[0])):
         base_rows(block, seen)
         score_rows(block, seen)
-    loss1[z * 2 + core] = finish((*range(per), *range(2 * per, 3 * per)), mine)
+    loss1[z * 2 + core] = finish(last_members, mine)
 
     ref = loss1.at[z * 2 + core]
     for dz in (4, 3, 5, 2, 6, 1, 7, 0):
@@ -397,13 +395,12 @@
     b1 = weighted.astype(jnp.bfloat16)
     b2 = (weighted - b1.astype(jnp.float32)).astype(jnp.bfloat16)
     r = wbuf[:, pl.ds(KB, MEM)].reshape(MEMBERS, COLS)
-    total = jnp.dot(b2, r, preferred_element_type=jnp.float32) + jnp.dot(b1, r, preferred_element_type=jnp.float32)
+    total = jnp.dot(jnp.concatenate([b2, b1], axis=0), r, preferred_element_type=jnp.float32)
+    total = total[:KB] + total[KB:]
     upd[...] = total * (1.0 / (MEMBERS * sigma_scale))
 
-    left_device(tokbuf.at[pl.ds(0, 12)], z_sent.at[0])
-    left_device(tokbuf.at[0, pl.ds(0, 4 * QUARTER - 2 * EXTRA)], z_sent.at[1])
-    left_device(tokbuf.at[pl.ds(0, 4)], t_sent.at[0])
-    left_device(tokbuf.at[0, pl.ds(0, 2 * (2 * EXTRA + MEM))], t_sent.at[1])
+    left_device(tokbuf, z_sent.at[0])
+    left_device(tokbuf.at[pl.ds(0, 2), pl.ds(0, HALF + EXTRA + MEM)], z_sent.at[1])
     left_device(wbuf.at[pl.ds(0, 28)], w_sent)
     @pl.when(middle)
     def _():
@@ -447,11 +444,10 @@
             pltpu.VMEM((16, 1, 128), f32),
             pltpu.VMEM((32, 1, 128), f32),
             dma((5,)),
-            dma((2,)), dma((2, 2, 7)),
-            dma((2,)), dma((3, 2)), dma((3,)),
-            dma(()), dma(()), dma((NYL,)), dma((2, 4)), dma((4,)), dma((4,)),
+            dma((2,)), dma((2, 2, 7)), dma((3,)), dma((3,)),
+            dma(()), dma(()), dma((NYL,)), dma((4,)), dma((4,)), dma((4,)),
             dma((3,)), dma((3,)),
-            pltpu.SemaphoreType.REGULAR((2, 2)),
+            pltpu.SemaphoreType.REGULAR((2,)),
         ],
         compiler_params=pltpu.CompilerParams(
             collective_id=0, has_side_effects=True, vmem_limit_bytes=56 * 1024 * 1024

time: 103 us -> 104 us (level)
  no operation moved by 1% of the time
where the time goes in v4:
time: 104 us; the launch traced here: 103 us
  Pallas kernels  103 us (99%)
    pallas_call x1, Pallas kernels, per_device(): pl.pallas_call(kernel, out_shape=(pltpu.VMEM((ROWS, COLS), bf), pltpu.VME...  102 us

profile of v4, /device:TPU:1, one launch (start us, length us, event | category | flops | bytes accessed | tf_op | source)
XLA Modules:
  0.0 103.4 jit_solution(2552951297324451574)
XLA Ops:
  0.6 101.8 %shard_map.68 = (bf16[512,512]{1,0:T(8,128)(2,1)S(1)}, f32[256,512]{1,0:T(8,128)S(1)}) custom-call(bf16[512,512]{1,0:T(8,128)(2,1)} %tok_hbm.1, bf16[256,512]{1,0:T(8,128)(2,1)} %w_hbm.1, bf16[16,512]{1,0:T(8,128)(2,1)} %left_hbm.1, bf16[16,512]{1,0:T(8,128)(2,1)} %right_hbm.1, bf16[512,512]{1,0:T(8,128)(2,1)} %tgt_hbm.1), custom_call_target="tpu_custom_call" | custom-call | tf_op jit(solution)/shard_map/pallas_call | solution.py:429
  102.4 1.0 shard_map.69

commit v5 on v4

--- a/solution.py
+++ b/solution.py
@@ -23,7 +23,7 @@
 MEM = 16
 TB = ROWS + MEM
 WB = KB + MEM
-LAST = 64
+LAST = 96
 EXTRA = 32
 HALF = 256
 WHALF = 128

time: 104 us -> 103 us (level)
  no operation moved by 1% of the time
where the time goes in v5:
time: 103 us
  Pallas kernels  102 us (99%)
    pallas_call x1, Pallas kernels, per_device(): pl.pallas_call(kernel, out_shape=(pltpu.VMEM((ROWS, COLS), bf), pltpu.VME...  101 us

profile of v5, /device:TPU:1, one launch (start us, length us, event | category | flops | bytes accessed | tf_op | source)
XLA Modules:
  0.0 103.0 jit_solution(12943185119082966005)
XLA Ops:
  0.6 101.4 %shard_map.68 = (bf16[512,512]{1,0:T(8,128)(2,1)S(1)}, f32[256,512]{1,0:T(8,128)S(1)}) custom-call(bf16[512,512]{1,0:T(8,128)(2,1)} %tok_hbm.1, bf16[256,512]{1,0:T(8,128)(2,1)} %w_hbm.1, bf16[16,512]{1,0:T(8,128)(2,1)} %left_hbm.1, bf16[16,512]{1,0:T(8,128)(2,1)} %right_hbm.1, bf16[512,512]{1,0:T(8,128)(2,1)} %tgt_hbm.1), custom_call_target="tpu_custom_call" | custom-call | tf_op jit(solution)/shard_map/pallas_call | solution.py:429
  102.0 1.0 shard_map.69

commit v6 on v5

--- a/solution.py
+++ b/solution.py
@@ -362,9 +362,6 @@
                 dev = (pop_of(yl, x, (core + dc) % 2), ((z + dz) % NZ) * 2 + yh)
                 remote(ref, ref, small_sent.at[1], small_got.at[1], dev).start()
 
-    got(leftbuf.at[pl.ds(0, NPOP - 1)], small_got.at[0])
-    left_t[...] = leftbuf[...].reshape(MEMBERS, KB).astype(jnp.float32).T
-
     got(loss1.at[pl.ds(0, 15)], small_got.at[1])
     row = loss1[0]
     for i in range(1, 16):
@@ -375,6 +372,9 @@
         for dx in (2, 1, 3, 0):
             if dy or dx:
                 remote(ref, ref, small_sent.at[2], small_got.at[2], at_yx((y + dy) % NY, (x + dx) % NX)).start()
+    got(leftbuf.at[pl.ds(0, NPOP - 1)], small_got.at[0])
+    left_t[...] = leftbuf[...].reshape(MEMBERS, KB).astype(jnp.float32).T
+
     got(loss2.at[pl.ds(0, 31)], small_got.at[2])
 
     losses = []

time: 103 us -> 103 us (level)
  no operation moved by 1% of the time
where the time goes in v6:
time: 103 us
  Pallas kernels  102 us (99%)
    pallas_call x1, Pallas kernels, per_device(): pl.pallas_call(kernel, out_shape=(pltpu.VMEM((ROWS, COLS), bf), pltpu.VME...  101 us

profile of v6, /device:TPU:1, one launch (start us, length us, event | category | flops | bytes accessed | tf_op | source)
XLA Modules:
  0.0 103.0 jit_solution(7033413034352137742)
XLA Ops:
  0.6 101.4 %shard_map.68 = (bf16[512,512]{1,0:T(8,128)(2,1)S(1)}, f32[256,512]{1,0:T(8,128)S(1)}) custom-call(bf16[512,512]{1,0:T(8,128)(2,1)} %tok_hbm.1, bf16[256,512]{1,0:T(8,128)(2,1)} %w_hbm.1, bf16[16,512]{1,0:T(8,128)(2,1)} %left_hbm.1, bf16[16,512]{1,0:T(8,128)(2,1)} %right_hbm.1, bf16[512,512]{1,0:T(8,128)(2,1)} %tgt_hbm.1), custom_call_target="tpu_custom_call" | custom-call | tf_op jit(solution)/shard_map/pallas_call | solution.py:429
  102.0 1.0 shard_map.69

commit v7 on v6

--- a/solution.py
+++ b/solution.py
@@ -341,8 +341,9 @@
         return mine
 
     mate(2, z)
+    score_rows(before, top)
     zevent(1, 5)
-    for block, seen, scored in ((before, rests[1], (top, rests[1])), (after, rests[0], (rests[0],))):
+    for block, seen, scored in ((before, rests[1], (rests[1],)), (after, rests[0], (rests[0],))):
         base_rows(block, seen)
         for rows in scored:
             score_rows(block, rows)
@@ -416,11 +417,13 @@
 
 
 def write_out(hid, upd, hid_hbm, upd_hbm, sem):
-    copies = [pltpu.make_async_copy(hid, hid_hbm, sem.at[0]), pltpu.make_async_copy(upd, upd_hbm, sem.at[1])]
-    for c in copies:
-        c.start()
-    for c in copies:
-        c.wait()
+    for i, (src, dst) in enumerate(((upd, upd_hbm), (hid, hid_hbm))):
+        rows = src.shape[0] // 4
+        for n in range(4):
+            part = pl.ds(n * rows, rows)
+            pltpu.make_async_copy(src.at[part], dst.at[part], sem.at[i]).start()
+    pltpu.make_async_copy(upd, upd_hbm, sem.at[0]).wait()
+    pltpu.make_async_copy(hid, hid_hbm, sem.at[1]).wait()
 
 
 def per_device(tokens, weight, left, right, target):

time: 103 us -> 103 us (level)
  no operation moved by 1% of the time
where the time goes in v7:
time: 103 us
  Pallas kernels  102 us (99%)
    pallas_call x1, Pallas kernels, per_device(): pl.pallas_call(kernel, out_shape=(pltpu.VMEM((ROWS, COLS), bf), pltpu.VME...  101 us

profile of v7, /device:TPU:1, one launch (start us, length us, event | category | flops | bytes accessed | tf_op | source)
XLA Modules:
  0.0 103.0 jit_solution(6524918114937947932)
XLA Ops:
  0.6 101.4 %shard_map.68 = (bf16[512,512]{1,0:T(8,128)(2,1)S(1)}, f32[256,512]{1,0:T(8,128)S(1)}) custom-call(bf16[512,512]{1,0:T(8,128)(2,1)} %tok_hbm.1, bf16[256,512]{1,0:T(8,128)(2,1)} %w_hbm.1, bf16[16,512]{1,0:T(8,128)(2,1)} %left_hbm.1, bf16[16,512]{1,0:T(8,128)(2,1)} %right_hbm.1, bf16[512,512]{1,0:T(8,128)(2,1)} %tgt_hbm.1), custom_call_target="tpu_custom_call" | custom-call | tf_op jit(solution)/shard_map/pallas_call | solution.py:432
  102.0 1.0 shard_map.69
